TPU v7x, 32 devices: a whole 2x2x4 slice. The times are simulated.
32 devices in a mesh: expert: 16 (over z, y, core), tensor: 2 (over x).
Axes of the slice: x: 2, y: 2, z: 4, core: 2. Of those that a mesh axis runs over, the one named last changes fastest.
Arguments:
- tokens: bfloat16 [64, 256, 1280], P(('expert', 'tensor')), may hold values from -6 to 6
- slot_keys: bfloat16 [1280, 16], replicated, may hold values from -6 to 6
- logit_scale: float32 [], replicated, may hold values from 40 to 80
- w_in: bfloat16 [16, 1280, 3584], P('expert', None, 'tensor'), may hold values from -0.625 to 0.625
- b_in: bfloat16 [16, 3584], P('expert', 'tensor'), may hold values from -3 to 3
- w_out: bfloat16 [16, 3584, 1280], P('expert', 'tensor'), may hold values from -0.09375 to 0.09375
- b_out: bfloat16 [16, 1280], P('expert'), may hold values from -3 to 3
Outputs:
- mixed: bfloat16 [64, 256, 1280], P(('expert', 'tensor'))
All inputs are finite; a program needn't handle non-finite values.
Results may differ from a plain program's by a relative error of at most 0.0071.
Values may be sent and summed in bfloat16 or wider, within the bound.
A program may use at most 64 MiB of HBM per device.

v0:
```python
import jax
import jax.numpy as jnp
from jax import lax
from jax.sharding import PartitionSpec as P

EPS = 1e-06


def local(tokens, slot_keys, logit_scale, w_in, b_in, w_out, b_out):
    images, seq_len, width = tokens.shape
    slots = slot_keys.shape[1]
    row_sq = jnp.sum(jnp.square(tokens.astype(jnp.float32)), axis=2, keepdims=True)
    row_inv = lax.rsqrt(row_sq + EPS)
    key_sq = jnp.sum(jnp.square(slot_keys.astype(jnp.float32)), axis=0)
    key_inv = lax.rsqrt(key_sq + EPS)
    raw = jnp.dot(
        tokens.reshape(images * seq_len, width), slot_keys, preferred_element_type=jnp.float32
    )
    logits = logit_scale * row_inv * key_inv * raw.reshape(images, seq_len, slots)
    expo = jnp.exp(logits)
    dispatch = (expo / jnp.sum(expo, axis=1, keepdims=True)).astype(jnp.bfloat16)
    combine = (expo / jnp.sum(expo, axis=2, keepdims=True)).astype(jnp.bfloat16)
    slot_in = jnp.einsum(
        "ims,imd->isd", dispatch, tokens, preferred_element_type=jnp.float32
    ).astype(jnp.bfloat16)
    routed = lax.all_to_all(slot_in, "expert", split_axis=1, concat_axis=0, tiled=True)
    bias_wide = b_in.astype(jnp.float32)
    pre = (
        jnp.einsum(
            "rkd,kdf->rkf",
            lax.all_gather(routed, "tensor", axis=0, tiled=True),
            w_in,
            preferred_element_type=jnp.float32,
        )
        + bias_wide[None]
    )
    hidden = jax.nn.gelu(pre).astype(jnp.bfloat16)
    mine = lax.psum_scatter(
        jnp.einsum("rkf,kfd->rkd", hidden, w_out, preferred_element_type=jnp.float32),
        "tensor",
        scatter_dimension=0,
        tiled=True,
    )
    slot_out = (mine + b_out.astype(jnp.float32)[None]).astype(jnp.bfloat16)
    returned = lax.all_to_all(slot_out, "expert", split_axis=0, concat_axis=1, tiled=True)
    mixed = jnp.einsum("ims,isd->imd", combine, returned, preferred_element_type=jnp.float32)
    return mixed.astype(jnp.bfloat16)


def solution(mesh):
    placed = (
        P(("expert", "tensor"), None, None),
        P(),
        P(),
        P("expert", None, "tensor"),
        P("expert", "tensor"),
        P("expert", "tensor", None),
        P("expert", None),
    )
    return jax.shard_map(
        local,
        mesh=mesh,
        in_specs=placed,
        out_specs=P(("expert", "tensor"), None, None),
        check_vma=False,
    )
```

profile of v0, /device:TPU:0, one launch (start us, length us, event | category | flops | bytes accessed | tf_op | source)
XLA Modules:
  0.0 72.5 jit_solution(5864950734486424679)
XLA Ops:
  6.5 0.0 copy-start
  6.5 0.0 copy-start.1
  7.3 0.9 %multiply_reduce_fusion.1 = f32[16]{0:T(128)S(1)} fusion(bf16[1280,16]{0,1:T(8,128)(2,1)} %param.8), kind=kLoop, calls=%fused_computation.32 | loop fusion | flops 61424 | bytes 41024 | tf_op jit(solution)/shard_map/reduce_sum | solution.py:14
  8.2 1.7 %multiply_reduce_fusion = f32[2,256]{1,0:T(2,128)S(1)} fusion(bf16[2,256,1280]{2,1,0:T(8,128)(2,1)} %param.7), kind=kLoop, calls=%fused_computation.5 | loop fusion | flops 1965568 | bytes 1312768 | tf_op jit(solution)/shard_map/reduce_sum | solution.py:12
  9.9 1.8 %fusion.16 = f32[2,256,16]{1,2,0:T(8,128)S(1)} fusion(bf16[2,256,1280]{2,1,0:T(8,128)(2,1)} %param.7, bf16[1280,16]{0,1:T(8,128)(2,1)} %param.8, f32[16]{0:T(128)S(1)} %add_rsqrt_fusion, f32[2,256]{1,0:T(2,128)S(1)} %rsqrt_multiply_fusion), kind=kOutput, calls=%fused_computation.12 | convolution fusion | flops 20987904 | bytes 1386560 | tf_op jit(solution)/shard_map/dot_general | solution.py:16
  11.7 0.0 copy-done
  11.7 0.3 convolution_convert_fusion.1
  12.0 0.7 copy.13
  12.7 7.4 %all-to-all-start = ((bf16[2,16,1280]{2,0,1:T(2,128)(2,1)}), bf16[2,16,1280]{2,0,1:T(2,128)(2,1)S(1)}, u32[]{:S(2)}, u32[]{:S(2)}) async-start(bf16[2,16,1280]{2,0,1:T(2,128)(2,1)} %copy.13), calls=%async_computation | async-start | bytes 163840 | tf_op jit(solution)/shard_map/all_to_all | solution.py:26
  20.1 0.0 reduce-scatter.2.cloned.1.call-start
  20.2 0.0 copy-done.1
  20.2 7.0 %all-to-all-done = bf16[2,16,1280]{2,0,1:T(2,128)(2,1)S(1)} async-done(((bf16[2,16,1280]{2,0,1:T(2,128)(2,1)}), bf16[2,16,1280]{2,0,1:T(2,128)(2,1)S(1)}, u32[]{:S(2)}, u32[]{:S(2)}) %all-to-all-start) | async-done | bytes 81952 | tf_op jit(solution)/shard_map/all_to_all | solution.py:26
  27.3 5.1 %all_gather.3 = bf16[64,1,1280]{2,0,1:T(8,128)(2,1)S(1)} all-gather(bf16[32,1,1280]{2,0,1:T(8,128)(2,1)S(1)} %all_to_all.29), channel_id=1, replica_groups=mesh['expert'=16,'tensor'=2] {'tensor'}, dimensions={0}, use_global_device_ids=true | all-gather | bytes 245760 | tf_op jit(solution)/shard_map/all_gather | solution.py:31
  32.4 0.0 copy-start.2
  32.4 6.3 %fusion.4 = f32[64,1,1280]{2,0,1:T(8,128)} fusion(bf16[1,1792,1280]{2,1,0:T(8,128)(2,1)} %param.12, bf16[1,1280,1792]{2,1,0:T(8,128)(2,1)} %param.10, f32[1792]{0:T(1024)S(1)} %convert_reduce_fusion, bf16[64,1,1280]{2,0,1:T(8,128)(2,1)S(1)} %all_gather.3), kind=kOutput, calls=%fused_computation.6 | convolution fusion | flops 588349440 | bytes 9673728 | tf_op jit(solution)/shard_map/rkf,kfd->rkd/dot_general | solution.py:39
  38.7 0.0 reduce-scatter.2.cloned.1.call-update
  38.7 0.0 copy-done.2
  38.7 10.0 %reduce-scatter.2.cloned.1.call-done = f32[32,1,1280]{2,0,1:T(8,128)} async-done(((f32[64,1,1280]{2,0,1:T(8,128)}), f32[32,1,1280]{2,0,1:T(8,128)}) %reduce-scatter.2.cloned.1.call-update) | async-done | bytes 163856 | tf_op jit(solution)/shard_map/reduce_scatter | solution.py:38
  48.7 0.9 %add_convert_fusion = bf16[32,1,1280]{2,0,1:T(8,128)(2,1)S(1)} fusion(f32[32,1,1280]{2,0,1:T(8,128)} %reduce-scatter.2.cloned.1.call-done, f32[1280]{0:T(1024)S(1)} %convert_reduce_fusion.1), kind=kLoop, calls=%fused_computation.29 | loop fusion | flops 81920 | bytes 250880 | tf_op jit(solution)/shard_map/convert_element_type | solution.py:44
  49.7 0.5 broadcast.27
  50.2 0.7 reduce.5
  50.9 12.5 %all_to_all.36 = bf16[16,2,1280]{2,1,0:T(2,128)(2,1)S(1)} all-to-all(bf16[16,2,1280]{2,1,0:T(2,128)(2,1)S(1)} %reshape.50), channel_id=1, replica_groups=mesh['expert'=16,'tensor'=2] {'expert'}, dimensions={0} | all-to-all | bytes 163840 | tf_op jit(solution)/shard_map/all_to_all | solution.py:45
  63.4 0.1 reshape.51
  63.5 0.5 reduce.2
  64.0 1.6 %convolution_convert_fusion = bf16[2,256,1280]{2,1,0:T(8,128)(2,1)} fusion(bf16[16,2,1,1280]{3,1,0,2:T(2,128)(2,1)S(1)} %all_to_all.31, f32[2,256,16]{1,2,0:T(8,128)S(1)} %fusion.16), kind=kOutput, calls=%fused_computation.4 | convolution fusion | flops 21643792 | bytes 1425408 | tf_op jit(solution)/shard_map/ims,isd->imd/dot_general | solution.py:46
  (7 shorter events, 0.2 us)
Async XLA Ops:
  6.5 5.1 %copy-start = (bf16[2,256,1280]{2,1,0:T(8,128)(2,1)S(1)}, bf16[2,256,1280]{2,1,0:T(8,128)(2,1)}, u32[]{:S(2)}) copy-start(bf16[2,256,1280]{2,1,0:T(8,128)(2,1)} %param.7) | copy-start | bytes 3932164
  6.5 13.6 %copy-start.1 = (bf16[1,1792]{1,0:T(2,128)(2,1)S(1)}, bf16[1,1792]{1,0:T(2,128)(2,1)}, u32[]{:S(2)}) copy-start(bf16[1,1792]{1,0:T(2,128)(2,1)} %param.11) | copy-start | bytes 10756
  12.7 14.5 %all-to-all-start = ((bf16[2,16,1280]{2,0,1:T(2,128)(2,1)}), bf16[2,16,1280]{2,0,1:T(2,128)(2,1)S(1)}, u32[]{:S(2)}, u32[]{:S(2)}) async-start(bf16[2,16,1280]{2,0,1:T(2,128)(2,1)} %copy.13), calls=%async_computation | async-start | bytes 163840 | tf_op jit(solution)/shard_map/all_to_all | solution.py:26
  20.1 28.6 %reduce-scatter.2.cloned.1.call-start = ((), (), s32[]{:S(2)}) async-start(), calls=%async_computation.3 | async-start | bytes 491520 | tf_op jit(solution)/shard_map/reduce_scatter | solution.py:38
  32.4 6.3 %copy-start.2 = (bf16[1,1280]{1,0:T(2,128)(2,1)S(1)}, bf16[1,1280]{1,0:T(2,128)(2,1)}, u32[]{:S(2)}) copy-start(bf16[1,1280]{1,0:T(2,128)(2,1)} %param.13) | copy-start | bytes 7684
Sparse Core Ops, SparseCore 0:
  38.8 9.8 reduce-scatter.1
where the time goes:
time: 72.8 us; the launch traced here: 72.5 us
  blocking collectives  17.6 us (24%)
  waiting for transfers between devices  17.1 us (23%)
  between operations  14.3 us (20%)
  matrix products  9.99 us (14%)
  starting transfers between devices  7.46 us (10%)
  other arithmetic  4.67 us (6%)
  local copies, waits for them, and re-layouts  1.4 us (2%)
    all_to_all x1, blocking collectives, local(): lax.all_to_all(slot_out, 'expert', split_axis=0, concat_axis=1, tiled=True)  12.5 us
    reduce_scatter x1, waiting for transfers between devices, local(): lax.psum_scatter(jnp.einsum('rkf,kfd->rkd', hidden, w_out, preferred_elem...  10 us
    all_to_all x1, starting transfers between devices, local(): lax.all_to_all(slot_in, 'expert', split_axis=1, concat_axis=0, tiled=True)  7.41 us
    all_to_all x1, waiting for transfers between devices, local(): lax.all_to_all(slot_in, 'expert', split_axis=1, concat_axis=0, tiled=True)  7.02 us
    dot_general x1, matrix products, local(): jnp.einsum('rkf,kfd->rkd', hidden, w_out, preferred_element_type=jnp.floa...  6.26 us
    all_gather x1, blocking collectives, local(): lax.all_gather(routed, 'tensor', axis=0, tiled=True)  5.11 us
    dot_general x1, matrix products, local(): jnp.dot(tokens.reshape(images * seq_len, width), slot_keys, preferred_ele...  1.78 us
    reduce_sum x1, other arithmetic, local(): jnp.sum(jnp.square(tokens.astype(jnp.float32)), axis=2, keepdims=True)  1.65 us
  transfers between devices with their start and end apart: 2, of which 2 were waited for; matrix products, arithmetic and copies ran while one was open for 0% of the time, Pallas kernels for 0%

commit v1 on v0

--- a/solution.py
+++ b/solution.py
@@ -42,7 +42,12 @@
         tiled=True,
     )
     slot_out = (mine + b_out.astype(jnp.float32)[None]).astype(jnp.bfloat16)
-    returned = lax.all_to_all(slot_out, "expert", split_axis=0, concat_axis=1, tiled=True)
+    returned = jnp.concatenate(
+        lax.all_to_all(
+            jnp.stack(jnp.split(slot_out, lax.axis_size("expert"), axis=0)), "expert", 0, 0
+        ),
+        axis=1,
+    )
     mixed = jnp.einsum("ims,isd->imd", combine, returned, preferred_element_type=jnp.float32)
     return mixed.astype(jnp.bfloat16)
 

time: 72.8 us -> 71.3 us (0.979)
  other arithmetic: 4.67 us -> 3.55 us
    convert_element_type x2 -> x1, other arithmetic: 1.59 us -> 0.93 us  [local(): slot_out = (mine + b_out.astype(jnp.float32)[None]).astype(jnp.bfloat16)]
where the time goes in v1:
time: 71.3 us; the launch traced here: 71 us
  blocking collectives  17.6 us (25%)
  waiting for transfers between devices  17.1 us (24%)
  between operations  14.3 us (20%)
  matrix products  9.98 us (14%)
  starting transfers between devices  7.46 us (10%)
  other arithmetic  3.55 us (5%)
  local copies, waits for them, and re-layouts  1 us (1%)
    all_to_all x1, blocking collectives, local(): lax.all_to_all(jnp.stack(jnp.split(slot_out, lax.axis_size('expert'), axi...  12.5 us
    reduce_scatter x1, waiting for transfers between devices, local(): lax.psum_scatter(jnp.einsum('rkf,kfd->rkd', hidden, w_out, preferred_elem...  10 us
    all_to_all x1, starting transfers between devices, local(): lax.all_to_all(slot_in, 'expert', split_axis=1, concat_axis=0, tiled=True)  7.41 us
    all_to_all x1, waiting for transfers between devices, local(): lax.all_to_all(slot_in, 'expert', split_axis=1, concat_axis=0, tiled=True)  7.02 us
    dot_general x1, matrix products, local(): jnp.einsum('rkf,kfd->rkd', hidden, w_out, preferred_element_type=jnp.floa...  6.26 us
    all_gather x1, blocking collectives, local(): lax.all_gather(routed, 'tensor', axis=0, tiled=True)  5.11 us
    dot_general x1, matrix products, local(): jnp.dot(tokens.reshape(images * seq_len, width), slot_keys, preferred_ele...  1.78 us
    reduce_sum x1, other arithmetic, local(): jnp.sum(jnp.square(tokens.astype(jnp.float32)), axis=2, keepdims=True)  1.65 us
  transfers between devices with their start and end apart: 2, of which 2 were waited for; matrix products, arithmetic and copies ran while one was open for 0% of the time, Pallas kernels for 0%

profile of v1, /device:TPU:0, one launch (start us, length us, event | category | flops | bytes accessed | tf_op | source)
XLA Modules:
  0.0 71.0 jit_solution(13144493296330274649)
XLA Ops:
  6.5 0.0 copy-start
  6.5 0.0 copy-start.1
  7.3 0.9 %multiply_reduce_fusion.1 = f32[16]{0:T(128)S(1)} fusion(bf16[1280,16]{0,1:T(8,128)(2,1)} %param.8), kind=kLoop, calls=%fused_computation.31 | loop fusion | flops 61424 | bytes 41024 | tf_op jit(solution)/shard_map/reduce_sum | solution.py:14
  8.2 1.7 %multiply_reduce_fusion = f32[2,256]{1,0:T(2,128)S(1)} fusion(bf16[2,256,1280]{2,1,0:T(8,128)(2,1)} %param.7), kind=kLoop, calls=%fused_computation.5 | loop fusion | flops 1965568 | bytes 1312768 | tf_op jit(solution)/shard_map/reduce_sum | solution.py:12
  9.9 1.8 %fusion.16 = f32[2,256,16]{1,2,0:T(8,128)S(1)} fusion(bf16[2,256,1280]{2,1,0:T(8,128)(2,1)} %param.7, bf16[1280,16]{0,1:T(8,128)(2,1)} %param.8, f32[16]{0:T(128)S(1)} %add_rsqrt_fusion, f32[2,256]{1,0:T(2,128)S(1)} %rsqrt_multiply_fusion), kind=kOutput, calls=%fused_computation.12 | convolution fusion | flops 20987904 | bytes 1386560 | tf_op jit(solution)/shard_map/dot_general | solution.py:16
  11.7 0.0 copy-done
  11.7 0.3 convolution_convert_fusion.1
  12.0 0.7 %copy.11 = bf16[2,16,1280]{2,0,1:T(2,128)(2,1)} copy(bf16[2,16,1280]{2,1,0:T(8,128)(2,1)S(1)} %convolution_convert_fusion.1) | data formatting | bytes 163840 | tf_op jit(solution)/shard_map/convert_element_type | solution.py:25
  12.7 7.4 %all-to-all-start = ((bf16[2,16,1280]{2,0,1:T(2,128)(2,1)}), bf16[2,16,1280]{2,0,1:T(2,128)(2,1)S(1)}, u32[]{:S(2)}, u32[]{:S(2)}) async-start(bf16[2,16,1280]{2,0,1:T(2,128)(2,1)} %copy.11), calls=%async_computation | async-start | bytes 163840 | tf_op jit(solution)/shard_map/all_to_all | solution.py:26
  20.1 0.0 reduce-scatter.2.cloned.1.call-start
  20.2 0.0 copy-done.1
  20.2 7.0 %all-to-all-done = bf16[2,16,1280]{2,0,1:T(2,128)(2,1)S(1)} async-done(((bf16[2,16,1280]{2,0,1:T(2,128)(2,1)}), bf16[2,16,1280]{2,0,1:T(2,128)(2,1)S(1)}, u32[]{:S(2)}, u32[]{:S(2)}) %all-to-all-start) | async-done | bytes 81952 | tf_op jit(solution)/shard_map/all_to_all | solution.py:26
  27.3 5.1 %all_gather.3 = bf16[64,1,1280]{2,0,1:T(8,128)(2,1)S(1)} all-gather(bf16[32,1,1280]{2,0,1:T(8,128)(2,1)S(1)} %all_to_all.19), channel_id=1, replica_groups=mesh['expert'=16,'tensor'=2] {'tensor'}, dimensions={0}, use_global_device_ids=true | all-gather | bytes 245760 | tf_op jit(solution)/shard_map/all_gather | solution.py:31
  32.4 0.0 copy-start.2
  32.4 6.3 %fusion.4 = f32[64,1,1280]{2,0,1:T(8,128)} fusion(bf16[1,1792,1280]{2,1,0:T(8,128)(2,1)} %param.12, bf16[1,1280,1792]{2,1,0:T(8,128)(2,1)} %param.10, f32[1792]{0:T(1024)S(1)} %convert_reduce_fusion, bf16[64,1,1280]{2,0,1:T(8,128)(2,1)S(1)} %all_gather.3), kind=kOutput, calls=%fused_computation.6 | convolution fusion | flops 588349440 | bytes 9673728 | tf_op jit(solution)/shard_map/rkf,kfd->rkd/dot_general | solution.py:39
  38.7 0.0 reduce-scatter.2.cloned.1.call-update
  38.7 0.0 copy-done.2
  38.7 10.0 %reduce-scatter.2.cloned.1.call-done = f32[32,1,1280]{2,0,1:T(8,128)} async-done(((f32[64,1,1280]{2,0,1:T(8,128)}), f32[32,1,1280]{2,0,1:T(8,128)}) %reduce-scatter.2.cloned.1.call-update) | async-done | bytes 163856 | tf_op jit(solution)/shard_map/reduce_scatter | solution.py:38
  48.7 0.9 %add_convert_fusion = bf16[32,1,1280]{2,0,1:T(8,128)(2,1)S(1)} fusion(f32[32,1,1280]{2,0,1:T(8,128)} %reduce-scatter.2.cloned.1.call-done, f32[1280]{0:T(1024)S(1)} %convert_reduce_fusion.1), kind=kLoop, calls=%fused_computation.29 | loop fusion | flops 81920 | bytes 250880 | tf_op jit(solution)/shard_map/convert_element_type | solution.py:44
  50.0 12.5 %all_to_all.23 = bf16[16,2,1,1280]{3,1,2,0:T(2,128)(2,1)S(1)} all-to-all(bf16[16,2,1,1280]{3,1,2,0:T(2,128)(2,1)S(1)} %constant_dynamic-update-slice_fusion), channel_id=1, replica_groups=mesh['expert'=16,'tensor'=2] {'expert'}, dimensions={0} | all-to-all | bytes 163840 | tf_op jit(solution)/shard_map/all_to_all | solution.py:46
  62.5 1.6 %convolution_convert_fusion = bf16[2,256,1280]{2,1,0:T(8,128)(2,1)} fusion(bf16[2,16,1280]{2,0,1:T(2,128)(2,1)S(1)} %bitcast.141, f32[2,256,16]{1,2,0:T(8,128)S(1)} %fusion.16), kind=kOutput, calls=%fused_computation.4 | convolution fusion | flops 21643792 | bytes 1425408 | tf_op jit(solution)/shard_map/ims,isd->imd/dot_general | solution.py:51
  (21 shorter events, 0.3 us)
Async XLA Ops:
  6.5 5.1 %copy-start = (bf16[2,256,1280]{2,1,0:T(8,128)(2,1)S(1)}, bf16[2,256,1280]{2,1,0:T(8,128)(2,1)}, u32[]{:S(2)}) copy-start(bf16[2,256,1280]{2,1,0:T(8,128)(2,1)} %param.7) | copy-start | bytes 3932164
  6.5 13.6 %copy-start.1 = (bf16[1,1792]{1,0:T(2,128)(2,1)S(1)}, bf16[1,1792]{1,0:T(2,128)(2,1)}, u32[]{:S(2)}) copy-start(bf16[1,1792]{1,0:T(2,128)(2,1)} %param.11) | copy-start | bytes 10756
  12.7 14.5 %all-to-all-start = ((bf16[2,16,1280]{2,0,1:T(2,128)(2,1)}), bf16[2,16,1280]{2,0,1:T(2,128)(2,1)S(1)}, u32[]{:S(2)}, u32[]{:S(2)}) async-start(bf16[2,16,1280]{2,0,1:T(2,128)(2,1)} %copy.11), calls=%async_computation | async-start | bytes 163840 | tf_op jit(solution)/shard_map/all_to_all | solution.py:26
  20.1 28.6 %reduce-scatter.2.cloned.1.call-start = ((), (), s32[]{:S(2)}) async-start(), calls=%async_computation.3 | async-start | bytes 491520 | tf_op jit(solution)/shard_map/reduce_scatter | solution.py:38
  32.4 6.3 %copy-start.2 = (bf16[1,1280]{1,0:T(2,128)(2,1)S(1)}, bf16[1,1280]{1,0:T(2,128)(2,1)}, u32[]{:S(2)}) copy-start(bf16[1,1280]{1,0:T(2,128)(2,1)} %param.13) | copy-start | bytes 7684
Sparse Core Ops, SparseCore 0:
  38.8 9.8 reduce-scatter.1
